TPU v7x, 256 devices: a whole 4x4x8 slice. The times are simulated.
256 devices in a mesh: rows: 32 (over y, x, core), rhs: 8 (over z).
Axes of the slice: x: 4, y: 4, z: 8, core: 2. Of those that a mesh axis runs over, the one named last changes fastest.
Arguments:
- sources: bfloat16 [131072, 4096], P('rows', 'rhs'), may hold values from -6 to 6
- near_blocks: bfloat16 [512, 3, 256, 256], P('rows'), may hold values from -0.21875 to 0.21875
- near_list: int32 [512, 3], P('rows'), may hold values from 0 to 511, as said below
- source_basis: bfloat16 [512, 256, 32], P('rows'), may hold values from -0.375 to 0.375
- target_basis: bfloat16 [512, 256, 32], P('rows'), may hold values from -0.375 to 0.375
- transfer_fine: bfloat16 [896, 32, 32], P('rows'), may hold values from -0.875 to 0.875
- transfer_coarse: bfloat16 [128, 32, 32], P('rhs'), may hold values from -0.875 to 0.875
- couple_fine: bfloat16 [896, 3, 32, 32], P('rows'), may hold values from -0.625 to 0.625
- couple_coarse: bfloat16 [128, 3, 32, 32], P('rhs'), may hold values from -0.625 to 0.625
- far_fine: int32 [896, 3], P('rows'), may hold values from 0 to 511, as said below
- far_coarse: int32 [128, 3], replicated, may hold values from -1 to 63, as said below
Outputs:
- potentials: bfloat16 [131072, 4096], P('rows', 'rhs')
Inputs may be any that keep to these rules, and one draw needn't show every extreme that they name: `near_list`: row t lists the leaf clusters t - 1, t and t + 1 modulo 512 in some order. `far_fine`: row d * 28 + o + i belongs to cluster d * m + i of the level with n = m * 32 clusters, where (o, m) is (0, 16), (16, 8) or (24, 4). It lists, in some order, the three clusters of that level that are children of the cyclic neighbours of the cluster's parent and not cyclic neighbours of the cluster: for cluster j with parent p = j // 2, the clusters 2p - 2, 2p + 2, 2p + 3 if j is even and 2p - 2, 2p - 1, 2p + 3 if j is odd, modulo n. `far_coarse`: row n + j for n = 8, 16, ..., 64 lists, in some order, the three far clusters of cluster j of the level with n clusters by the rule of far_fine. Row 4 + j holds (j + 2) modulo 4 in slot 0 and -1 in slots 1 and 2. Rows 0 to 3 hold -1.
All inputs are finite; a program needn't handle non-finite values.
Results may differ from a plain program's by a relative error of at most 0.012.
Values may be sent and summed in bfloat16 or wider, within the bound.
A program may use at most 128 MiB of HBM per device.

v0:
```python
import jax
import jax.numpy as jnp
from jax import lax
from jax.sharding import PartitionSpec as P


def padded_2(cells, sides, width):
    for axis, dim in sides:
        count = lax.axis_size(axis)
        head = lax.slice_in_dim(cells, 0, width, axis=dim)
        tail = lax.slice_in_dim(cells, cells.shape[dim] - width, cells.shape[dim], axis=dim)
        cells = jnp.concatenate(
            [
                lax.ppermute(tail, axis, [(i, (i + 1) % count) for i in range(count)]),
                cells,
                lax.ppermute(head, axis, [((i + 1) % count, i) for i in range(count)]),
            ],
            axis=dim,
        )
    return cells


def from_everyone(shard, axis):
    copies = jnp.broadcast_to(shard, (lax.axis_size(axis), *shard.shape))
    return lax.all_to_all(copies, axis, split_axis=0, concat_axis=0, tiled=True)


def joined_along(pieces, dim):
    pieces = jnp.moveaxis(pieces, 0, dim)
    dims = pieces.shape
    return pieces.reshape(*dims[:dim], dims[dim] * dims[dim + 1], *dims[dim + 2 :])


def gather_directly(shard, axis, dim):
    pieces = from_everyone(shard, axis)
    return joined_along(pieces, dim)


def sent_together(arrays, axis, dim, along):
    columns = [a.reshape(*a.shape[:along], -1) for a in arrays]
    both = jnp.concatenate(columns, axis=along)
    whole, at, finished = (gather_directly(both, axis, dim), 0, [])
    for a, column in zip(arrays, columns):
        slab = whole[..., at : at + column.shape[along]]
        finished.append(slab.reshape(*slab.shape[:along], *a.shape[along:]))
        at += column.shape[along]
    return tuple(finished)


def couple_masked(moments, blocks, partners):
    valid = partners >= 0
    picked = moments[jnp.maximum(partners, 0)]
    picked = jnp.where(valid[:, :, None, None], picked, jnp.zeros_like(picked))
    return jnp.einsum("nsab,nsbr->nar", blocks, picked, preferred_element_type=jnp.float32)


def routed_blocks(blocks, offset, wanted):
    chosen = jnp.zeros_like(blocks[:, 0])
    for slot in range(3):
        match = (offset[:, slot] == wanted)[:, None, None]
        chosen = jnp.where(match, blocks[:, slot], chosen)
    return chosen


def couple_window(moments, blocks, partners, position, row_count):
    clusters = moments.shape[0]
    level_size = clusters * row_count
    window = padded_2(moments, (("rows", 0),), 3)
    targets = position * clusters + jnp.arange(clusters, dtype=jnp.int32)
    offset = (partners - targets[:, None] + level_size // 2) % level_size - level_size // 2
    coupled = jnp.zeros((clusters, moments.shape[1], moments.shape[2]), jnp.float32)
    for wanted in (-3, -2, 2, 3):
        chosen = routed_blocks(blocks, offset, wanted)
        shifted = window[3 + wanted : 3 + wanted + clusters]
        coupled = coupled + jnp.einsum(
            "nab,nbr->nar", chosen, shifted, preferred_element_type=jnp.float32
        )
    return coupled


def lift(moments, transfer):
    clusters, rank, width = moments.shape
    product = jnp.einsum("nab,nar->nbr", transfer, moments, preferred_element_type=jnp.float32)
    return product.reshape(clusters // 2, 2, rank, width).sum(axis=1).astype(jnp.bfloat16)


def lower(parent, transfer, coupled):
    spread = jnp.repeat(parent, 2, axis=0)
    carried = jnp.einsum("nab,nbr->nar", transfer, spread, preferred_element_type=jnp.float32)
    return (coupled + carried).astype(jnp.bfloat16)


def coarse_pass(moments, transfer_all, couple_all, far_all):
    clusters = moments.shape[0]
    depth = clusters.bit_length() - 3
    upward = [moments]
    for step in range(depth):
        moments = lift(moments, transfer_all[clusters : 2 * clusters])
        clusters = clusters // 2
        upward.append(moments)
    downward = moments
    for step in range(depth + 1):
        coupled = couple_masked(
            upward[depth - step],
            couple_all[clusters : 2 * clusters],
            far_all[clusters : 2 * clusters],
        )
        if step == 0:
            downward = coupled.astype(jnp.bfloat16)
        else:
            downward = lower(downward, transfer_all[clusters : 2 * clusters], coupled)
        clusters = clusters * 2
    return downward


def body(
    sources,
    near_blocks,
    near_list,
    source_basis,
    target_basis,
    transfer_fine,
    transfer_coarse,
    couple_fine,
    couple_coarse,
    far_fine,
    far_coarse,
):
    count = near_blocks.shape[0]
    leaf = near_blocks.shape[2]
    width = sources.shape[1]
    row_count = lax.axis_size("rows")
    position = lax.axis_index("rows")
    all_leaves = count * row_count
    padded = padded_2(sources, (("rows", 0),), leaf)
    neighbours = padded.reshape(count + 2, leaf, width)
    targets = position * count + jnp.arange(count, dtype=jnp.int32)
    offset = (near_list - targets[:, None] + all_leaves // 2) % all_leaves - all_leaves // 2
    near_part = jnp.zeros((count, leaf, width), jnp.float32)
    for wanted in (-1, 0, 1):
        chosen = routed_blocks(near_blocks, offset, wanted)
        shifted = neighbours[1 + wanted : 1 + wanted + count]
        near_part = near_part + jnp.einsum(
            "npq,nqr->npr", chosen, shifted, preferred_element_type=jnp.float32
        )
    shaped = sources.reshape(count, leaf, width)
    moments = jnp.einsum(
        "npk,npr->nkr", source_basis, shaped, preferred_element_type=jnp.float32
    ).astype(jnp.bfloat16)
    level_counts = [count, count // 2, count // 4]
    firsts = [0, count, count + count // 2]
    upward = [moments]
    for level in range(3):
        moments = lift(moments, transfer_fine[firsts[level] : firsts[level] + level_counts[level]])
        upward.append(moments)
    tables = sent_together((transfer_coarse, couple_coarse), "rhs", 0, 1)
    columns = lax.all_to_all(moments, "rows", split_axis=2, concat_axis=0, tiled=True)
    result = coarse_pass(columns, tables[0], tables[1], far_coarse)
    parents = lax.all_to_all(result, "rows", split_axis=0, concat_axis=2, tiled=True)
    downward = parents
    for level in (2, 1, 0):
        first = firsts[level]
        last = first + level_counts[level]
        coupled = couple_window(
            upward[level], couple_fine[first:last], far_fine[first:last], position, row_count
        )
        downward = lower(downward, transfer_fine[first:last], coupled)
    far_part = jnp.einsum(
        "npk,nkr->npr", target_basis, downward, preferred_element_type=jnp.float32
    )
    return (far_part + near_part).astype(jnp.bfloat16).reshape(count * leaf, width)


def solution(mesh):
    in_specs = (
        P("rows", "rhs"),
        P("rows", None, None, None),
        P("rows", None),
        P("rows", None, None),
        P("rows", None, None),
        P("rows", None, None),
        P("rhs", None, None),
        P("rows", None, None, None),
        P("rhs", None, None, None),
        P("rows", None),
        P(),
    )
    out_specs = P("rows", "rhs")
    return jax.shard_map(body, mesh=mesh, in_specs=in_specs, out_specs=out_specs, check_vma=False)
```

profile of v0, /device:TPU:1, one launch (start us, length us, event | category | flops | bytes accessed | tf_op | source)
XLA Modules:
  0.0 168.6 jit_solution(6814324130455730087)
XLA Ops:
  0.1 3.2 %convolution_convert_fusion = bf16[16,32,512]{2,1,0:T(8,128)(2,1)S(1)} fusion(bf16[16,256,32]{1,2,0:T(8,128)(2,1)} %param.14, bf16[16,256,512]{2,1,0:T(8,128)(2,1)} %bitcast.431), kind=kOutput, calls=%fused_computation.51 | convolution fusion | flops 134479872 | bytes 4980736 | tf_op jit(solution)/shard_map/npk,npr->nkr/dot_general | solution.py:147
  3.9 2.6 %collective-permute-start = (bf16[3,32,512]{2,1,0:T(8,128)(2,1)}, bf16[3,32,512]{2,1,0:T(8,128)(2,1)S(1)}, u32[]{:S(2)}, u32[]{:S(2)}) collective-permute-start(bf16[3,32,512]{2,1,0:T(8,128)(2,1)} %get-tuple-element.9), channel_id=1, source_target_pairs={{0,8},{8,16},{16,24},{24,32},{32,40},{40,48},{48,56},{56,64},{64,7... | collective-permute-start | bytes 294920 | tf_op jit(solution)/shard_map/ppermute | solution.py:14
  8.1 0.8 reshape.478
  9.0 8.5 %all-to-all-start.1 = ((bf16[32,2,512]{2,1,0:T(2,128)(2,1)}), bf16[32,2,512]{2,1,0:T(2,128)(2,1)S(1)}, u32[]{:S(2)}, u32[]{:S(2)}) async-start(bf16[32,2,512]{2,1,0:T(2,128)(2,1)} %reshape.478), calls=%async_computation.1 | async-start | bytes 131072 | tf_op jit(solution)/shard_map/all_to_all | solution.py:157
  17.5 0.7 fusion.300
  18.2 1.6 collective-permute-start.4
  20.5 3.8 %collective-permute-start.3 = (bf16[3,32,512]{2,1,0:T(8,128)(2,1)S(1)}, bf16[3,32,512]{2,1,0:T(8,128)(2,1)S(1)}, u32[]{:S(2)}, u32[]{:S(2)}) collective-permute-start(bf16[3,32,512]{2,1,0:T(8,128)(2,1)S(1)} %get-tuple-element.12), channel_id=1, source_target_pairs={{8,0},{16,8},{24,16},{32,24},{40,32},{48,40},{56,48},{64,56},{72,6... | collective-permute-start | bytes 294920 | tf_op jit(solution)/shard_map/ppermute | solution.py:16
  25.0 1.8 %fusion.297 = (bf16[256,512]{1,0:T(8,128)(2,1)}, bf16[256,512]{1,0:T(8,128)(2,1)S(1)}) fusion(bf16[4096,512]{1,0:T(8,128)(2,1)} %param.11), kind=kLoop, calls=%fused_computation.404 | loop fusion | bytes 1048576 | tf_op jit(solution)/shard_map/slice | solution.py:10
  34.4 0.7 copy.112
  36.8 8.7 %fusion.7 = f32[16,256,512]{2,1,0:T(8,128)} fusion(bf16[16,256,512]{2,1,0:T(8,128)(2,1)} %bitcast.432, pred[16]{0:T(512)(128)(4,1)S(1)} %get-tuple-element.19, pred[16]{0:T(512)(128)(4,1)S(1)} %get-tuple-element.17, pred[16]{0:T(512)(128)(4,1)S(1)} %get-tuple-element.16, bf16[16,3,256,256]{3,2,1,0:T(8,128)(2,1)} %param.12), kind=kOutput, calls=%fused_computation.17 | convolution fusion | flops 1076887552 | bytes 18874416 | tf_op jit(solution)/shard_map/npq,nqr->npr/dot_general | solution.py:143
  45.5 1.1 broadcast_in_dim.421
  46.6 6.8 %all-to-all-start = ((bf16[8,16,4096]{2,1,0:T(8,128)(2,1)}), bf16[8,16,4096]{2,1,0:T(8,128)(2,1)}, u32[]{:S(2)}, u32[]{:S(2)}) async-start(bf16[8,16,4096]{2,1,0:T(8,128)(2,1)} %broadcast_in_dim.421), calls=%async_computation | async-start | bytes 2097152 | tf_op jit(solution)/shard_map/all_to_all | solution.py:25
  53.6 1.6 gather_fusion
  55.4 2.0 %fusion.80 = f32[8,32,512]{2,1,0:T(8,128)} fusion(bf16[3,32,512]{2,1,0:T(8,128)(2,1)S(1)} %collective-permute-done.3, bf16[8,32,512]{2,1,0:T(8,128)(2,1)S(1)} %bitcast_reduce_fusion, pred[8]{0:T(512)(128)(4,1)S(1)} %get-tuple-element.45, pred[8]{0:T(512)(128)(4,1)S(1)} %get-tuple-element.42, pred[8]{0:T(512)(128)(4,1)S(1)} %get-tuple-element.39, ...), kind=kOutput, calls=%fused_computation.111 | convolution fusion | flops 8544256 | bytes 1081368 | tf_op jit(solution)/shard_map/nab,nbr->nar/dot_general | solution.py:75
  58.0 1.6 fusion.68
  59.7 2.0 %fusion.76 = f32[8,32,512]{2,1,0:T(8,128)} fusion(bf16[8,32,512]{2,1,0:T(8,128)(2,1)S(1)} %bitcast_reduce_fusion, bf16[3,32,512]{2,1,0:T(8,128)(2,1)S(1)} %collective-permute-done.3, pred[8]{0:T(512)(128)(4,1)S(1)} %copy-done.42, pred[8]{0:T(512)(128)(4,1)S(1)} %copy-done.41, pred[8]{0:T(512)(128)(4,1)S(1)} %copy-done.40, bf16[28,3,32,32]{3,2,1,0:T(8,128)(2,1)} %param.18), kind=kOutput, calls=%fused_computation.108 | convolution fusion | flops 8544256 | bytes 1081368 | tf_op jit(solution)/shard_map/nab,nbr->nar/dot_general | solution.py:75
  61.7 1.1 collective-permute-start.6
  62.8 2.0 %fusion.82 = f32[8,32,512]{2,1,0:T(8,128)} fusion(bf16[8,32,512]{2,1,0:T(8,128)(2,1)S(1)} %bitcast_reduce_fusion, bf16[3,32,512]{2,1,0:T(8,128)(2,1)S(1)} %collective-permute-done.2, pred[8]{0:T(512)(128)(4,1)S(1)} %get-tuple-element.43, pred[8]{0:T(512)(128)(4,1)S(1)} %get-tuple-element.40, pred[8]{0:T(512)(128)(4,1)S(1)} %get-tuple-element.37, ...), kind=kOutput, calls=%fused_computation.114 | convolution fusion | flops 8544256 | bytes 1081368 | tf_op jit(solution)/shard_map/nab,nbr->nar/dot_general | solution.py:75
  64.8 1.7 %fusion.92 = f32[4,32,512]{2,1,0:T(8,128)} fusion(bf16[3,32,512]{2,1,0:T(8,128)(2,1)S(1)} %collective-permute-done.5, bf16[4,32,512]{2,1,0:T(8,128)(2,1)S(1)} %bitcast_reduce_fusion.1, pred[4]{0:T(512)(128)(4,1)S(1)} %get-tuple-element.57, pred[4]{0:T(512)(128)(4,1)S(1)} %get-tuple-element.54, pred[4]{0:T(512)(128)(4,1)S(1)} %get-tuple-element.51, ...), kind=kOutput, calls=%fused_computation.129 | convolution fusion | flops 4272128 | bytes 589836 | tf_op jit(solution)/shard_map/nab,nbr->nar/dot_general | solution.py:75
  66.5 2.4 %fusion.63 = f32[16,32,512]{2,1,0:T(8,128)} fusion(bf16[16,32,512]{2,1,0:T(8,128)(2,1)S(1)} %convolution_convert_fusion, bf16[3,32,512]{2,1,0:T(8,128)(2,1)} %copy-done.15, pred[16]{0:T(512)(128)(4,1)S(1)} %copy-done.45, pred[16]{0:T(512)(128)(4,1)S(1)} %copy-done.44, pred[16]{0:T(512)(128)(4,1)S(1)} %copy-done.43, bf16[28,3,32,32]{3,2,1,0:T(8,128)(2,1)} %param.18), kind=kOutput, calls=%fused_computation.90 | convolution fusion | flops 17088512 | bytes 2064432 | tf_op jit(solution)/shard_map/nab,nbr->nar/dot_general | solution.py:75
  68.9 1.7 %fusion.88 = f32[4,32,512]{2,1,0:T(8,128)} fusion(bf16[4,32,512]{2,1,0:T(8,128)(2,1)S(1)} %bitcast_reduce_fusion.1, bf16[3,32,512]{2,1,0:T(8,128)(2,1)S(1)} %collective-permute-done.5, pred[4]{0:T(512)(128)(4,1)S(1)} %get-tuple-element.56, pred[4]{0:T(512)(128)(4,1)S(1)} %get-tuple-element.53, pred[4]{0:T(512)(128)(4,1)S(1)} %get-tuple-element.50, ...), kind=kOutput, calls=%fused_computation.126 | convolution fusion | flops 4272128 | bytes 589836 | tf_op jit(solution)/shard_map/nab,nbr->nar/dot_general | solution.py:75
  70.6 1.8 %fusion.94 = f32[4,32,512]{2,1,0:T(8,128)} fusion(bf16[4,32,512]{2,1,0:T(8,128)(2,1)S(1)} %bitcast_reduce_fusion.1, bf16[3,32,512]{2,1,0:T(8,128)(2,1)S(1)} %collective-permute-done.4, pred[4]{0:T(512)(128)(4,1)S(1)} %get-tuple-element.55, pred[4]{0:T(512)(128)(4,1)S(1)} %get-tuple-element.52, pred[4]{0:T(512)(128)(4,1)S(1)} %get-tuple-element.49, ...), kind=kOutput, calls=%fused_computation.132 | convolution fusion | flops 4272128 | bytes 589836 | tf_op jit(solution)/shard_map/nab,nbr->nar/dot_general | solution.py:75
  72.5 2.4 %fusion.70 = f32[16,32,512]{2,1,0:T(8,128)} fusion(bf16[16,32,512]{2,1,0:T(8,128)(2,1)S(1)} %convolution_convert_fusion, bf16[3,32,512]{2,1,0:T(8,128)(2,1)S(1)} %collective-permute-done, pred[16]{0:T(512)(128)(4,1)S(1)} %copy-done.30, pred[16]{0:T(512)(128)(4,1)S(1)} %copy-done.29, pred[16]{0:T(512)(128)(4,1)S(1)} %copy-done.28, ...), kind=kOutput, calls=%fused_computation.96 | convolution fusion | flops 17088512 | bytes 2064432 | tf_op jit(solution)/shard_map/nab,nbr->nar/dot_general | solution.py:75
  74.9 3.6 %pad_maximum_fusion = (bf16[4096,512]{1,0:T(8,128)(2,1)}, bf16[4096,512]{1,0:T(8,128)(2,1)}) fusion(bf16[256,512]{1,0:T(8,128)(2,1)S(1)} %collective-permute-done.7, bf16[4096,512]{1,0:T(8,128)(2,1)S(1)} %copy-done.1, bf16[256,512]{1,0:T(8,128)(2,1)S(1)} %collective-permute-done.6), kind=kLoop, calls=%fused_computation.7 | loop fusion | flops 16777216 | bytes 13107200 | tf_op jit(solution)/shard_map/concatenate | solution.py:12
  78.5 4.2 %all-to-all-done = bf16[8,16,4096]{2,1,0:T(8,128)(2,1)} async-done(((bf16[8,16,4096]{2,1,0:T(8,128)(2,1)}), bf16[8,16,4096]{2,1,0:T(8,128)(2,1)}, u32[]{:S(2)}, u32[]{:S(2)}) %all-to-all-start) | async-done | bytes 1048608 | tf_op jit(solution)/shard_map/all_to_all | solution.py:25
  82.7 0.7 slice.455
  83.4 0.8 slice.456
  84.2 0.8 slice.453
  85.0 0.8 slice.454
  85.8 0.8 slice.451
  86.6 1.5 slice.452
  88.2 0.9 slice.449
  89.1 1.6 slice.450
  90.7 1.8 %slice.448 = bf16[64,3072]{1,0:T(8,128)(2,1)} slice(bf16[128,4096]{1,0:T(8,128)(2,1)} %bitcast.50), slice={[64:128], [1024:4096]} | slice | bytes 786432 | tf_op jit(solution)/shard_map/slice | solution.py:105
  92.5 0.7 slice.404
  93.2 0.8 slice.406
  94.1 0.8 copy.119
  95.0 0.9 slice.401
  96.0 1.7 %copy.129 = bf16[64,32,32]{2,1,0:T(8,128)(2,1)S(1)} copy(bf16[64,32,32]{0,2,1:T(8,128)(2,1)} %bitcast.441) | data formatting | bytes 262144 | tf_op jit(solution)/shard_map/slice | solution.py:111
  98.4 1.0 bitcast_reduce_fusion.6
  99.4 1.3 gather_fusion.3
  100.7 1.4 gather_fusion.2
  102.1 1.5 gather_fusion.1
  103.6 2.0 %slice.396 = bf16[16,3,32,32]{3,2,1,0:T(8,128)(2,1)} reshape(bf16[16,3072]{1,0:T(8,128)(2,1)} %slice.452) | data formatting | bytes 196608 | tf_op jit(solution)/shard_map/slice | solution.py:105
  105.6 2.2 %copy.111 = bf16[64,3072]{0,1:T(8,128)(2,1)} copy(bf16[64,3072]{1,0:T(8,128)(2,1)} %slice.448) | data formatting | bytes 786432 | tf_op jit(solution)/shard_map/slice | solution.py:105
  107.9 2.4 %slice.391 = bf16[32,3,32,32]{3,2,1,0:T(8,128)(2,1)} reshape(bf16[32,3072]{1,0:T(8,128)(2,1)} %slice.450) | data formatting | bytes 393216 | tf_op jit(solution)/shard_map/slice | solution.py:105
  110.2 3.1 %copy.118 = bf16[64,3,32,32]{3,2,1,0:T(8,128)(2,1)} copy(bf16[64,3,32,32]{0,3,2,1:T(8,128)(2,1)} %bitcast.438) | data formatting | bytes 786432 | tf_op jit(solution)/shard_map/slice | solution.py:105
  113.3 1.3 gather_fusion.4
  114.6 1.2 fusion.56
  115.8 1.2 convolution_bitcast_fusion.6
  117.1 1.0 fusion.55
  118.1 1.4 convolution_bitcast_fusion.5
  119.8 1.6 convolution_bitcast_fusion.4
  121.7 1.9 %convolution_bitcast_fusion.2 = f32[64,32,16]{1,2,0:T(8,128)S(1)} fusion(bf16[64,3,32,32]{3,2,1,0:T(8,128)(2,1)S(1)} %copy-done.3, bf16[64,3,32,16]{2,3,1,0:T(8,128)(2,1)} %bitcast.437, pred[64,3]{1,0:T(8,128)(4,1)S(1)} %copy-done.17), kind=kOutput, calls=%fused_computation.53 | convolution fusion | flops 6389760 | bytes 721088 | tf_op jit(solution)/shard_map/nsab,nsbr->nar/dot_general | solution.py:54
  124.0 0.9 reshape.480
  124.8 6.3 %all-to-all-start.2 = ((bf16[32,2,512]{2,1,0:T(2,128)(2,1)}), bf16[32,2,512]{2,1,0:T(2,128)(2,1)S(1)}, u32[]{:S(2)}, u32[]{:S(2)}) async-start(bf16[32,2,512]{2,1,0:T(2,128)(2,1)} %reshape.480), calls=%async_computation.2 | async-start | bytes 131072 | tf_op jit(solution)/shard_map/all_to_all | solution.py:159
  131.2 8.6 %fusion.3 = f32[16,256,512]{2,1,0:T(8,128)} fusion(bf16[16,256,512]{2,1,0:T(8,128)(2,1)} %bitcast.436, pred[16]{0:T(512)(128)(4,1)S(1)} %copy-done.37, pred[16]{0:T(512)(128)(4,1)S(1)} %copy-done.38, pred[16]{0:T(512)(128)(4,1)S(1)} %copy-done.39, bf16[16,3,256,256]{3,2,1,0:T(8,128)(2,1)} %param.12), kind=kOutput, calls=%fused_computation.14 | convolution fusion | flops 1076887552 | bytes 18874416 | tf_op jit(solution)/shard_map/npq,nqr->npr/dot_general | solution.py:143
  140.2 0.9 convolution_bitcast_fusion.3
  141.2 1.4 fusion.53
  142.7 1.0 convolution_bitcast_fusion.1
  143.8 1.6 fusion.48
  145.5 1.2 convolution_bitcast_fusion
  146.7 6.6 %fusion.46 = f32[16,512,256]{1,2,0:T(8,128)} fusion(bf16[16,256,32]{1,2,0:T(8,128)(2,1)S(1)} %copy-done, f32[16,32,512]{2,1,0:T(8,128)S(1)} %convolution_bitcast_fusion, f32[16,32,512]{2,1,0:T(8,128)S(1)} %fusion.68, f32[16,32,512]{2,1,0:T(8,128)} %fusion.63, f32[16,32,512]{2,1,0:T(8,128)} %fusion.70, bf16[3,32,512]{2,1,0:T(8,128)(2,1)S(1)} %copy-done.7, ...), kind=kOutput, calls=%fused_computation.58 | convolution fusion | flops 152616960 | bytes 13860912 | tf_op jit(solution)/shard_map/npk,nkr->npr/dot_general | solution.py:168
  153.3 15.3 %fusion = bf16[16,256,512]{2,1,0:T(8,128)(2,1)} fusion(f32[16,512,256]{1,2,0:T(8,128)} %fusion.46, f32[16,256,512]{2,1,0:T(8,128)} %fusion.3, f32[16,256,512]{2,1,0:T(8,128)} %fusion.7, bf16[16,256,512]{2,1,0:T(8,128)(2,1)} %bitcast.435, pred[16]{0:T(512)(128)(4,1)S(1)} %copy-done.36, pred[16]{0:T(512)(128)(4,1)S(1)} %copy-done.35, ...), kind=kOutput, calls=%fused_computation.6 | convolution fusion | flops 1085276160 | bytes 39845936 | tf_op jit(solution)/shard_map/npq,nqr->npr/dot_general | solution.py:143
  (175 shorter events, 16.4 us)
Async XLA Ops:
  0.0 146.6 %copy-start = (bf16[16,256,32]{1,2,0:T(8,128)(2,1)S(1)}, bf16[16,256,32]{1,2,0:T(8,128)(2,1)}, u32[]{:S(2)}) copy-start(bf16[16,256,32]{1,2,0:T(8,128)(2,1)} %param.15) | copy-start | bytes 786436
  0.0 7.1 %copy-start.5 = (bf16[28,32,32]{2,1,0:T(8,128)(2,1)S(1)}, bf16[28,32,32]{2,1,0:T(8,128)(2,1)}, u32[]{:S(2)}) copy-start(bf16[28,32,32]{2,1,0:T(8,128)(2,1)} %param.16) | copy-start | bytes 172036
  0.0 24.3 %copy-start.13 = (s32[128,3]{0,1:T(4,128)S(1)}, s32[128,3]{0,1:T(4,128)}, u32[]{:S(2)}) copy-start(s32[128,3]{0,1:T(4,128)} %param.21) | copy-start | bytes 4612
  0.0 28.8 %copy-start.16 = (s32[28,3]{0,1:T(4,128)S(1)}, s32[28,3]{0,1:T(4,128)}, u32[]{:S(2)}) copy-start(s32[28,3]{0,1:T(4,128)} %param.20) | copy-start | bytes 1012
  0.0 31.2 %copy-start.24 = (s32[16,3]{0,1:T(4,128)S(1)}, s32[16,3]{0,1:T(4,128)}, u32[]{:S(2)}) copy-start(s32[16,3]{0,1:T(4,128)} %param.13) | copy-start | bytes 580
  0.0 36.1 %copy-start.14 = (bf16[16,32,32]{2,1,0:T(8,128)(2,1)S(1)}, bf16[16,32,32]{2,1,0:T(8,128)(2,1)}, u32[]{:S(2)}) copy-start(bf16[16,32,32]{2,1,0:T(8,128)(2,1)} %param.17) | copy-start | bytes 98308
  0.0 36.3 %copy-start.12 = (bf16[16,3,32,32]{3,2,1,0:T(8,128)(2,1)S(1)}, bf16[16,3,32,32]{3,2,1,0:T(8,128)(2,1)}, u32[]{:S(2)}) copy-start(bf16[16,3,32,32]{3,2,1,0:T(8,128)(2,1)} %param.19) | copy-start | bytes 294916
  3.9 68.6 %collective-permute-start = (bf16[3,32,512]{2,1,0:T(8,128)(2,1)}, bf16[3,32,512]{2,1,0:T(8,128)(2,1)S(1)}, u32[]{:S(2)}, u32[]{:S(2)}) collective-permute-start(bf16[3,32,512]{2,1,0:T(8,128)(2,1)} %get-tuple-element.9), channel_id=1, source_target_pairs={{0,8},{8,16},{16,24},{24,32},{32,40},{40,48},{48,56},{56,64},{64,7... | collective-permute-start | bytes 294920 | tf_op jit(solution)/shard_map/ppermute | solution.py:14
  6.5 50.9 %collective-permute-start.1 = (bf16[3,32,512]{2,1,0:T(8,128)(2,1)S(1)}, bf16[3,32,512]{2,1,0:T(8,128)(2,1)S(1)}, u32[]{:S(2)}, u32[]{:S(2)}) collective-permute-start(bf16[3,32,512]{2,1,0:T(8,128)(2,1)S(1)} %get-tuple-element.10), channel_id=1, source_target_pairs={{8,0},{16,8},{24,16},{32,24},{40,32},{48,40},{56,48},{64,56},{72,6... | collective-permute-start | bytes 294920 | tf_op jit(solution)/shard_map/ppermute | solution.py:16
  9.0 36.5 %all-to-all-start.1 = ((bf16[32,2,512]{2,1,0:T(2,128)(2,1)}), bf16[32,2,512]{2,1,0:T(2,128)(2,1)S(1)}, u32[]{:S(2)}, u32[]{:S(2)}) async-start(bf16[32,2,512]{2,1,0:T(2,128)(2,1)} %reshape.478), calls=%async_computation.1 | async-start | bytes 131072 | tf_op jit(solution)/shard_map/all_to_all | solution.py:157
  18.2 52.4 %collective-permute-start.4 = (bf16[3,32,512]{2,1,0:T(8,128)(2,1)}, bf16[3,32,512]{2,1,0:T(8,128)(2,1)S(1)}, u32[]{:S(2)}, u32[]{:S(2)}) collective-permute-start(bf16[3,32,512]{2,1,0:T(8,128)(2,1)} %get-tuple-element.13), channel_id=1, source_target_pairs={{0,8},{8,16},{16,24},{24,32},{32,40},{40,48},{48,56},{56,64},{64,7... | collective-permute-start | bytes 294920 | tf_op jit(solution)/shard_map/ppermute | solution.py:14
  19.8 44.9 %collective-permute-start.5 = (bf16[3,32,512]{2,1,0:T(8,128)(2,1)}, bf16[3,32,512]{2,1,0:T(8,128)(2,1)S(1)}, u32[]{:S(2)}, u32[]{:S(2)}) collective-permute-start(bf16[3,32,512]{2,1,0:T(8,128)(2,1)} %get-tuple-element.14), channel_id=1, source_target_pairs={{8,0},{16,8},{24,16},{32,24},{40,32},{48,40},{56,48},{64,56},{72,6... | collective-permute-start | bytes 294920 | tf_op jit(solution)/shard_map/ppermute | solution.py:16
  20.5 34.8 %collective-permute-start.3 = (bf16[3,32,512]{2,1,0:T(8,128)(2,1)S(1)}, bf16[3,32,512]{2,1,0:T(8,128)(2,1)S(1)}, u32[]{:S(2)}, u32[]{:S(2)}) collective-permute-start(bf16[3,32,512]{2,1,0:T(8,128)(2,1)S(1)} %get-tuple-element.12), channel_id=1, source_target_pairs={{8,0},{16,8},{24,16},{32,24},{40,32},{48,40},{56,48},{64,56},{72,6... | collective-permute-start | bytes 294920 | tf_op jit(solution)/shard_map/ppermute | solution.py:16
  45.5 12.6 %copy-start.31 = (pred[16]{0:T(512)(128)(4,1)S(1)}, pred[16]{0:T(512)(128)(4,1)}, u32[]{:S(2)}) copy-start(pred[16]{0:T(512)(128)(4,1)} %get-tuple-element.27) | copy-start | bytes 52
  45.5 12.6 %copy-start.32 = (pred[16]{0:T(512)(128)(4,1)S(1)}, pred[16]{0:T(512)(128)(4,1)}, u32[]{:S(2)}) copy-start(pred[16]{0:T(512)(128)(4,1)} %get-tuple-element.30) | copy-start | bytes 52
  45.5 12.6 %copy-start.33 = (pred[16]{0:T(512)(128)(4,1)S(1)}, pred[16]{0:T(512)(128)(4,1)}, u32[]{:S(2)}) copy-start(pred[16]{0:T(512)(128)(4,1)} %get-tuple-element.33) | copy-start | bytes 52
  46.6 13.1 %copy-start.40 = (pred[8]{0:T(512)(128)(4,1)S(1)}, pred[8]{0:T(512)(128)(4,1)}, u32[]{:S(2)}) copy-start(pred[8]{0:T(512)(128)(4,1)} %get-tuple-element.38) | copy-start | bytes 28
  46.6 13.1 %copy-start.41 = (pred[8]{0:T(512)(128)(4,1)S(1)}, pred[8]{0:T(512)(128)(4,1)}, u32[]{:S(2)}) copy-start(pred[8]{0:T(512)(128)(4,1)} %get-tuple-element.41) | copy-start | bytes 28
  46.6 13.1 %copy-start.42 = (pred[8]{0:T(512)(128)(4,1)S(1)}, pred[8]{0:T(512)(128)(4,1)}, u32[]{:S(2)}) copy-start(pred[8]{0:T(512)(128)(4,1)} %get-tuple-element.44) | copy-start | bytes 28
  46.6 36.1 %all-to-all-start = ((bf16[8,16,4096]{2,1,0:T(8,128)(2,1)}), bf16[8,16,4096]{2,1,0:T(8,128)(2,1)}, u32[]{:S(2)}, u32[]{:S(2)}) async-start(bf16[8,16,4096]{2,1,0:T(8,128)(2,1)} %broadcast_in_dim.421), calls=%async_computation | async-start | bytes 2097152 | tf_op jit(solution)/shard_map/all_to_all | solution.py:25
  53.6 12.9 %copy-start.43 = (pred[16]{0:T(512)(128)(4,1)S(1)}, pred[16]{0:T(512)(128)(4,1)}, u32[]{:S(2)}) copy-start(pred[16]{0:T(512)(128)(4,1)} %get-tuple-element.26) | copy-start | bytes 52
  53.6 12.9 %copy-start.44 = (pred[16]{0:T(512)(128)(4,1)S(1)}, pred[16]{0:T(512)(128)(4,1)}, u32[]{:S(2)}) copy-start(pred[16]{0:T(512)(128)(4,1)} %get-tuple-element.29) | copy-start | bytes 52
  53.6 12.9 %copy-start.45 = (pred[16]{0:T(512)(128)(4,1)S(1)}, pred[16]{0:T(512)(128)(4,1)}, u32[]{:S(2)}) copy-start(pred[16]{0:T(512)(128)(4,1)} %get-tuple-element.32) | copy-start | bytes 52
  55.3 17.2 %copy-start.28 = (pred[16]{0:T(512)(128)(4,1)S(1)}, pred[16]{0:T(512)(128)(4,1)}, u32[]{:S(2)}) copy-start(pred[16]{0:T(512)(128)(4,1)} %get-tuple-element.25) | copy-start | bytes 52
  55.3 17.2 %copy-start.29 = (pred[16]{0:T(512)(128)(4,1)S(1)}, pred[16]{0:T(512)(128)(4,1)}, u32[]{:S(2)}) copy-start(pred[16]{0:T(512)(128)(4,1)} %get-tuple-element.28) | copy-start | bytes 52
  55.3 17.2 %copy-start.30 = (pred[16]{0:T(512)(128)(4,1)S(1)}, pred[16]{0:T(512)(128)(4,1)}, u32[]{:S(2)}) copy-start(pred[16]{0:T(512)(128)(4,1)} %get-tuple-element.31) | copy-start | bytes 52
  55.3 6.4 %collective-permute-start.2 = (bf16[3,32,512]{2,1,0:T(8,128)(2,1)}, bf16[3,32,512]{2,1,0:T(8,128)(2,1)S(1)}, u32[]{:S(2)}, u32[]{:S(2)}) collective-permute-start(bf16[3,32,512]{2,1,0:T(8,128)(2,1)} %get-tuple-element.11), channel_id=1, source_target_pairs={{0,8},{8,16},{16,24},{24,32},{32,40},{40,48},{48,56},{56,64},{64,7... | collective-permute-start | bytes 294920 | tf_op jit(solution)/shard_map/ppermute | solution.py:14
  57.4 0.7 copy-start.15
  57.4 17.5 %collective-permute-start.7 = (bf16[256,512]{1,0:T(8,128)(2,1)}, bf16[256,512]{1,0:T(8,128)(2,1)S(1)}, u32[]{:S(2)}, u32[]{:S(2)}) collective-permute-start(bf16[256,512]{1,0:T(8,128)(2,1)} %get-tuple-element.7), channel_id=1, source_target_pairs={{8,0},{16,8},{24,16},{32,24},{40,32},{48,40},{56,48},{64,56},{72,6... | collective-permute-start | bytes 786440 | tf_op jit(solution)/shard_map/ppermute | solution.py:16
  58.0 16.8 %copy-start.1 = (bf16[4096,512]{1,0:T(8,128)(2,1)S(1)}, bf16[4096,512]{1,0:T(8,128)(2,1)}, u32[]{:S(2)}) copy-start(bf16[4096,512]{1,0:T(8,128)(2,1)} %param.11) | copy-start | bytes 12582916
  61.7 16.8 %copy-start.8 = (bf16[3,32,512]{2,1,0:T(8,128)(2,1)}, bf16[3,32,512]{2,1,0:T(8,128)(2,1)S(1)}, u32[]{:S(2)}) copy-start(bf16[3,32,512]{2,1,0:T(8,128)(2,1)S(1)} %collective-permute-done.2) | copy-start | bytes 294916
  61.7 13.2 %collective-permute-start.6 = (bf16[256,512]{1,0:T(8,128)(2,1)S(1)}, bf16[256,512]{1,0:T(8,128)(2,1)S(1)}, u32[]{:S(2)}, u32[]{:S(2)}) collective-permute-start(bf16[256,512]{1,0:T(8,128)(2,1)S(1)} %get-tuple-element.8), channel_id=1, source_target_pairs={{0,8},{8,16},{16,24},{24,32},{32,40},{40,48},{48,56},{56,64},{64,7... | collective-permute-start | bytes 786440 | tf_op jit(solution)/shard_map/ppermute | solution.py:14
  70.6 7.9 %copy-start.10 = (bf16[3,32,512]{2,1,0:T(8,128)(2,1)}, bf16[3,32,512]{2,1,0:T(8,128)(2,1)S(1)}, u32[]{:S(2)}) copy-start(bf16[3,32,512]{2,1,0:T(8,128)(2,1)S(1)} %collective-permute-done.4) | copy-start | bytes 294916
  72.4 6.1 %copy-start.6 = (bf16[3,32,512]{2,1,0:T(8,128)(2,1)}, bf16[3,32,512]{2,1,0:T(8,128)(2,1)S(1)}, u32[]{:S(2)}) copy-start(bf16[3,32,512]{2,1,0:T(8,128)(2,1)S(1)} %collective-permute-done) | copy-start | bytes 294916
  103.6 16.1 %copy-start.4 = (bf16[96,32,16]{1,2,0:T(8,128)(2,1)S(1)}, bf16[96,32,16]{1,2,0:T(8,128)(2,1)}, u32[]{:S(2)}) copy-start(bf16[96,32,16]{1,2,0:T(8,128)(2,1)} %gather_fusion.1) | copy-start | bytes 294916
  114.6 7.0 %copy-start.3 = (bf16[64,3,32,32]{3,2,1,0:T(8,128)(2,1)S(1)}, bf16[64,3,32,32]{3,2,1,0:T(8,128)(2,1)}, u32[]{:S(2)}) copy-start(bf16[64,3,32,32]{3,2,1,0:T(8,128)(2,1)} %copy.118) | copy-start | bytes 1179652
  114.6 7.0 %copy-start.17 = (pred[64,3]{1,0:T(8,128)(4,1)S(1)}, pred[64,3]{1,0:T(8,128)(4,1)}, u32[]{:S(2)}) copy-start(pred[64,3]{1,0:T(8,128)(4,1)} %copy.112) | copy-start | bytes 580
  119.5 11.6 %copy-start.37 = (pred[16]{0:T(512)(128)(4,1)S(1)}, pred[16]{0:T(512)(128)(4,1)}, u32[]{:S(2)}) copy-start(pred[16]{0:T(512)(128)(4,1)} %get-tuple-element.21) | copy-start | bytes 52
  119.5 11.6 %copy-start.38 = (pred[16]{0:T(512)(128)(4,1)S(1)}, pred[16]{0:T(512)(128)(4,1)}, u32[]{:S(2)}) copy-start(pred[16]{0:T(512)(128)(4,1)} %get-tuple-element.22) | copy-start | bytes 52
  119.6 11.6 %copy-start.39 = (pred[16]{0:T(512)(128)(4,1)S(1)}, pred[16]{0:T(512)(128)(4,1)}, u32[]{:S(2)}) copy-start(pred[16]{0:T(512)(128)(4,1)} %get-tuple-element.23) | copy-start | bytes 52
  124.8 15.0 %all-to-all-start.2 = ((bf16[32,2,512]{2,1,0:T(2,128)(2,1)}), bf16[32,2,512]{2,1,0:T(2,128)(2,1)S(1)}, u32[]{:S(2)}, u32[]{:S(2)}) async-start(bf16[32,2,512]{2,1,0:T(2,128)(2,1)} %reshape.480), calls=%async_computation.2 | async-start | bytes 131072 | tf_op jit(solution)/shard_map/all_to_all | solution.py:159
  131.1 10.1 %copy-start.11 = (bf16[3,32,512]{2,1,0:T(8,128)(2,1)S(1)}, bf16[3,32,512]{2,1,0:T(8,128)(2,1)}, u32[]{:S(2)}) copy-start(bf16[3,32,512]{2,1,0:T(8,128)(2,1)} %copy-done.10) | copy-start | bytes 294916
  131.1 10.1 %copy-start.21 = (pred[4]{0:T(512)(128)(4,1)S(1)}, pred[4]{0:T(512)(128)(4,1)}, u32[]{:S(2)}) copy-start(pred[4]{0:T(512)(128)(4,1)} %get-tuple-element.48) | copy-start | bytes 16
  131.1 10.1 %copy-start.22 = (pred[4]{0:T(512)(128)(4,1)S(1)}, pred[4]{0:T(512)(128)(4,1)}, u32[]{:S(2)}) copy-start(pred[4]{0:T(512)(128)(4,1)} %get-tuple-element.58) | copy-start | bytes 16
  131.1 10.1 %copy-start.23 = (pred[4]{0:T(512)(128)(4,1)S(1)}, pred[4]{0:T(512)(128)(4,1)}, u32[]{:S(2)}) copy-start(pred[4]{0:T(512)(128)(4,1)} %get-tuple-element.59) | copy-start | bytes 16
  139.8 3.9 %copy-start.2 = (f32[8,32,512]{2,1,0:T(8,128)S(1)}, f32[8,32,512]{2,1,0:T(8,128)}, u32[]{:S(2)}) copy-start(f32[8,32,512]{2,1,0:T(8,128)} %fusion.80) | copy-start | bytes 1572868
  139.8 3.9 %copy-start.9 = (bf16[3,32,512]{2,1,0:T(8,128)(2,1)S(1)}, bf16[3,32,512]{2,1,0:T(8,128)(2,1)}, u32[]{:S(2)}) copy-start(bf16[3,32,512]{2,1,0:T(8,128)(2,1)} %copy-done.8) | copy-start | bytes 294916
  139.8 3.9 %copy-start.25 = (pred[8]{0:T(512)(128)(4,1)S(1)}, pred[8]{0:T(512)(128)(4,1)}, u32[]{:S(2)}) copy-start(pred[8]{0:T(512)(128)(4,1)} %get-tuple-element.36) | copy-start | bytes 28
  139.8 4.0 %copy-start.26 = (pred[8]{0:T(512)(128)(4,1)S(1)}, pred[8]{0:T(512)(128)(4,1)}, u32[]{:S(2)}) copy-start(pred[8]{0:T(512)(128)(4,1)} %get-tuple-element.46) | copy-start | bytes 28
  139.8 4.0 %copy-start.27 = (pred[8]{0:T(512)(128)(4,1)S(1)}, pred[8]{0:T(512)(128)(4,1)}, u32[]{:S(2)}) copy-start(pred[8]{0:T(512)(128)(4,1)} %get-tuple-element.47) | copy-start | bytes 28
  140.2 6.5 %copy-start.7 = (bf16[3,32,512]{2,1,0:T(8,128)(2,1)S(1)}, bf16[3,32,512]{2,1,0:T(8,128)(2,1)}, u32[]{:S(2)}) copy-start(bf16[3,32,512]{2,1,0:T(8,128)(2,1)} %copy-done.6) | copy-start | bytes 294916
  140.2 6.5 %copy-start.18 = (pred[16]{0:T(512)(128)(4,1)S(1)}, pred[16]{0:T(512)(128)(4,1)}, u32[]{:S(2)}) copy-start(pred[16]{0:T(512)(128)(4,1)} %get-tuple-element.24) | copy-start | bytes 52
  140.2 6.5 %copy-start.19 = (pred[16]{0:T(512)(128)(4,1)S(1)}, pred[16]{0:T(512)(128)(4,1)}, u32[]{:S(2)}) copy-start(pred[16]{0:T(512)(128)(4,1)} %get-tuple-element.34) | copy-start | bytes 52
  140.2 6.5 %copy-start.20 = (pred[16]{0:T(512)(128)(4,1)S(1)}, pred[16]{0:T(512)(128)(4,1)}, u32[]{:S(2)}) copy-start(pred[16]{0:T(512)(128)(4,1)} %get-tuple-element.35) | copy-start | bytes 52
  146.7 6.6 %copy-start.34 = (pred[16]{0:T(512)(128)(4,1)S(1)}, pred[16]{0:T(512)(128)(4,1)}, u32[]{:S(2)}) copy-start(pred[16]{0:T(512)(128)(4,1)} %get-tuple-element.15) | copy-start | bytes 52
  146.7 6.6 %copy-start.35 = (pred[16]{0:T(512)(128)(4,1)S(1)}, pred[16]{0:T(512)(128)(4,1)}, u32[]{:S(2)}) copy-start(pred[16]{0:T(512)(128)(4,1)} %get-tuple-element.18) | copy-start | bytes 52
  146.7 6.6 %copy-start.36 = (pred[16]{0:T(512)(128)(4,1)S(1)}, pred[16]{0:T(512)(128)(4,1)}, u32[]{:S(2)}) copy-start(pred[16]{0:T(512)(128)(4,1)} %get-tuple-element.20) | copy-start | bytes 52
where the time goes:
time: 170 us; the launch traced here: 169 us
  matrix products  77.7 us (46%)
  local copies, waits for them, and re-layouts  44.4 us (26%)
  starting transfers between devices  32 us (19%)
  other arithmetic  9.4 us (6%)
  waiting for transfers between devices  4.23 us (2%)
    dot_general x3, matrix products, body(): jnp.einsum('npq,nqr->npr', chosen, shifted, preferred_element_type=jnp.fl...  32.6 us
    dot_general x11, matrix products, couple_window(): jnp.einsum('nab,nbr->nar', chosen, shifted, preferred_element_type=jnp.fl...  20.6 us
    slice x11, local copies, waits for them, and re-layouts, coarse_pass(): couple_all[clusters:2 * clusters]  17.8 us
    all_to_all x1, starting transfers between devices, body(): lax.all_to_all(moments, 'rows', split_axis=2, concat_axis=0, tiled=True)  8.54 us
    dot_general x5, matrix products, couple_masked(): jnp.einsum('nsab,nsbr->nar', blocks, picked, preferred_element_type=jnp.f...  7.33 us
    gather x5, local copies, waits for them, and re-layouts, couple_masked(): picked = moments[jnp.maximum(partners, 0)]  7.18 us
    slice x9, local copies, waits for them, and re-layouts, coarse_pass(): downward = lower(downward, transfer_all[clusters:2 * clusters], coupled)  6.86 us
    all_to_all x1, starting transfers between devices, from_everyone(): return lax.all_to_all(copies, axis, split_axis=0, concat_axis=0, tiled=True)  6.79 us
  transfers between devices with their start and end apart: 11, of which 1 were waited for; matrix products, arithmetic and copies ran while one was open for 34% of the time, Pallas kernels for 0%

commit v1 on v0

--- a/solution.py
+++ b/solution.py
@@ -154,7 +154,15 @@
         moments = lift(moments, transfer_fine[firsts[level] : firsts[level] + level_counts[level]])
         upward.append(moments)
     tables = sent_together((transfer_coarse, couple_coarse), "rhs", 0, 1)
-    columns = lax.all_to_all(moments, "rows", split_axis=2, concat_axis=0, tiled=True)
+    columns = jnp.concatenate(
+        lax.all_to_all(
+            jnp.stack(jnp.split(moments, lax.axis_size("rows"), axis=2), axis=0),
+            axis_name="rows",
+            split_axis=0,
+            concat_axis=0,
+        ),
+        axis=0,
+    )
     result = coarse_pass(columns, tables[0], tables[1], far_coarse)
     parents = lax.all_to_all(result, "rows", split_axis=0, concat_axis=2, tiled=True)
     downward = parents

time: 170 us -> 172 us (1.012)
  local copies, waits for them, and re-layouts: 44.4 us -> 46.8 us
  starting transfers between devices: 32 us -> 33.9 us
    all_to_all x1, starting transfers between devices: 8.54 us -> 3.63 us  [body(): lax.all_to_all(jnp.stack(jnp.split(moments, lax.axis_size('rows'), axis=2...]
    ppermute x4, starting transfers between devices: 5.03 us -> 9.68 us  [padded_2(): lax.ppermute(head, axis, [((i + 1) % count, i) for i in range(count)])]
    unnamed x96 -> x103, local copies, waits for them, and re-layouts: 2.25 us -> 5.18 us
where the time goes in v1:
time: 172 us; the launch traced here: 170 us
  matrix products  77.5 us (45%)
  local copies, waits for them, and re-layouts  46.8 us (27%)
  starting transfers between devices  33.9 us (20%)
  other arithmetic  8.18 us (5%)
  waiting for transfers between devices  2.83 us (2%)
    dot_general x3, matrix products, body(): jnp.einsum('npq,nqr->npr', chosen, shifted, preferred_element_type=jnp.fl...  32.6 us
    dot_general x11, matrix products, couple_window(): jnp.einsum('nab,nbr->nar', chosen, shifted, preferred_element_type=jnp.fl...  20.5 us
    slice x11, local copies, waits for them, and re-layouts, coarse_pass(): couple_all[clusters:2 * clusters]  17.8 us
    ppermute x4, starting transfers between devices, padded_2(): lax.ppermute(head, axis, [((i + 1) % count, i) for i in range(count)])  9.68 us
    all_to_all x1, starting transfers between devices, body(): lax.all_to_all(result, 'rows', split_axis=0, concat_axis=2, tiled=True)  7.48 us
    dot_general x5, matrix products, couple_masked(): jnp.einsum('nsab,nsbr->nar', blocks, picked, preferred_element_type=jnp.f...  7.33 us
    gather x5, local copies, waits for them, and re-layouts, couple_masked(): picked = moments[jnp.maximum(partners, 0)]  7.21 us
    slice x9, local copies, waits for them, and re-layouts, coarse_pass(): downward = lower(downward, transfer_all[clusters:2 * clusters], coupled)  6.87 us
  transfers between devices with their start and end apart: 11, of which 1 were waited for; matrix products, arithmetic and copies ran while one was open for 34% of the time, Pallas kernels for 0%

profile of v1, /device:TPU:1, one launch (start us, length us, event | category | flops | bytes accessed | tf_op | source)
XLA Modules:
  0.0 170.0 jit_solution(18112974687398505836)
XLA Ops:
  0.0 3.1 %convolution_convert_fusion = bf16[16,32,512]{2,1,0:T(8,128)(2,1)S(1)} fusion(bf16[16,256,32]{1,2,0:T(8,128)(2,1)} %param.14, bf16[16,256,512]{2,1,0:T(8,128)(2,1)} %bitcast.556), kind=kOutput, calls=%fused_computation.51 | convolution fusion | flops 134479872 | bytes 4980736 | tf_op jit(solution)/shard_map/npk,npr->nkr/dot_general | solution.py:147
  3.2 2.7 %collective-permute-start = (bf16[3,32,512]{2,1,0:T(8,128)(2,1)S(1)}, bf16[3,32,512]{2,1,0:T(8,128)(2,1)S(1)}, u32[]{:S(2)}, u32[]{:S(2)}) collective-permute-start(bf16[3,32,512]{2,1,0:T(8,128)(2,1)S(1)} %get-tuple-element.9), channel_id=1, source_target_pairs={{0,8},{8,16},{16,24},{24,32},{32,40},{40,48},{48,56},{56,64},{64,7... | collective-permute-start | bytes 294920 | tf_op jit(solution)/shard_map/ppermute | solution.py:14
  7.9 1.1 collective-permute-start.4
  9.0 3.9 %collective-permute-start.5 = (bf16[3,32,512]{2,1,0:T(8,128)(2,1)}, bf16[3,32,512]{2,1,0:T(8,128)(2,1)S(1)}, u32[]{:S(2)}, u32[]{:S(2)}) collective-permute-start(bf16[3,32,512]{2,1,0:T(8,128)(2,1)} %get-tuple-element.14), channel_id=1, source_target_pairs={{8,0},{16,8},{24,16},{32,24},{40,32},{48,40},{56,48},{64,56},{72,6... | collective-permute-start | bytes 294920 | tf_op jit(solution)/shard_map/ppermute | solution.py:16
  13.5 5.1 %collective-permute-start.3 = (bf16[3,32,512]{2,1,0:T(8,128)(2,1)S(1)}, bf16[3,32,512]{2,1,0:T(8,128)(2,1)S(1)}, u32[]{:S(2)}, u32[]{:S(2)}) collective-permute-start(bf16[3,32,512]{2,1,0:T(8,128)(2,1)S(1)} %get-tuple-element.12), channel_id=1, source_target_pairs={{8,0},{16,8},{24,16},{32,24},{40,32},{48,40},{56,48},{64,56},{72,6... | collective-permute-start | bytes 294920 | tf_op jit(solution)/shard_map/ppermute | solution.py:16
  21.5 0.9 reshape.482
  22.4 3.6 %all-to-all-start.1 = ((bf16[32,2,512]{2,1,0:T(2,128)(2,1)}), bf16[32,2,512]{2,1,0:T(2,128)(2,1)S(1)}, u32[]{:S(2)}, u32[]{:S(2)}) async-start(bf16[32,2,512]{2,1,0:T(2,128)(2,1)} %reshape.482), calls=%async_computation.1 | async-start | bytes 131072 | tf_op jit(solution)/shard_map/all_to_all | solution.py:158
  26.8 1.8 %fusion.297 = (bf16[256,512]{1,0:T(8,128)(2,1)}, bf16[256,512]{1,0:T(8,128)(2,1)}) fusion(bf16[4096,512]{1,0:T(8,128)(2,1)} %param.11), kind=kLoop, calls=%fused_computation.468 | loop fusion | bytes 1048576 | tf_op jit(solution)/shard_map/slice | solution.py:10
  37.3 8.7 %fusion.7 = f32[16,256,512]{2,1,0:T(8,128)} fusion(bf16[16,256,512]{2,1,0:T(8,128)(2,1)} %bitcast.557, pred[16]{0:T(512)(128)(4,1)S(1)} %get-tuple-element.19, pred[16]{0:T(512)(128)(4,1)S(1)} %get-tuple-element.17, pred[16]{0:T(512)(128)(4,1)S(1)} %get-tuple-element.16, bf16[16,3,256,256]{3,2,1,0:T(8,128)(2,1)} %param.12), kind=kOutput, calls=%fused_computation.17 | convolution fusion | flops 1076887552 | bytes 18874416 | tf_op jit(solution)/shard_map/npq,nqr->npr/dot_general | solution.py:143
  46.0 1.1 broadcast_in_dim.421
  47.1 6.5 %all-to-all-start = ((bf16[8,16,4096]{2,1,0:T(8,128)(2,1)}), bf16[8,16,4096]{2,1,0:T(8,128)(2,1)}, u32[]{:S(2)}, u32[]{:S(2)}) async-start(bf16[8,16,4096]{2,1,0:T(8,128)(2,1)} %broadcast_in_dim.421), calls=%async_computation | async-start | bytes 2097152 | tf_op jit(solution)/shard_map/all_to_all | solution.py:25
  53.7 1.6 gather_fusion
  55.4 1.8 %collective-permute-start.2 = (bf16[3,32,512]{2,1,0:T(8,128)(2,1)}, bf16[3,32,512]{2,1,0:T(8,128)(2,1)S(1)}, u32[]{:S(2)}, u32[]{:S(2)}) collective-permute-start(bf16[3,32,512]{2,1,0:T(8,128)(2,1)} %get-tuple-element.11), channel_id=1, source_target_pairs={{0,8},{8,16},{16,24},{24,32},{32,40},{40,48},{48,56},{56,64},{64,7... | collective-permute-start | bytes 294920 | tf_op jit(solution)/shard_map/ppermute | solution.py:14
  57.2 2.0 %fusion.80 = f32[8,32,512]{2,1,0:T(8,128)} fusion(bf16[3,32,512]{2,1,0:T(8,128)(2,1)S(1)} %collective-permute-done.3, bf16[8,32,512]{2,1,0:T(8,128)(2,1)S(1)} %bitcast_reduce_fusion, pred[8]{0:T(512)(128)(4,1)S(1)} %get-tuple-element.45, pred[8]{0:T(512)(128)(4,1)S(1)} %get-tuple-element.42, pred[8]{0:T(512)(128)(4,1)S(1)} %get-tuple-element.39, ...), kind=kOutput, calls=%fused_computation.111 | convolution fusion | flops 8544256 | bytes 1081368 | tf_op jit(solution)/shard_map/nab,nbr->nar/dot_general | solution.py:75
  59.8 1.6 fusion.68
  61.4 2.0 %fusion.76 = f32[8,32,512]{2,1,0:T(8,128)} fusion(bf16[8,32,512]{2,1,0:T(8,128)(2,1)S(1)} %bitcast_reduce_fusion, bf16[3,32,512]{2,1,0:T(8,128)(2,1)S(1)} %collective-permute-done.3, pred[8]{0:T(512)(128)(4,1)S(1)} %get-tuple-element.44, pred[8]{0:T(512)(128)(4,1)S(1)} %get-tuple-element.41, pred[8]{0:T(512)(128)(4,1)S(1)} %get-tuple-element.38, ...), kind=kOutput, calls=%fused_computation.108 | convolution fusion | flops 8544256 | bytes 1081368 | tf_op jit(solution)/shard_map/nab,nbr->nar/dot_general | solution.py:75
  63.4 1.1 collective-permute-start.6
  64.5 2.0 %fusion.82 = f32[8,32,512]{2,1,0:T(8,128)} fusion(bf16[8,32,512]{2,1,0:T(8,128)(2,1)S(1)} %bitcast_reduce_fusion, bf16[3,32,512]{2,1,0:T(8,128)(2,1)S(1)} %collective-permute-done.2, pred[8]{0:T(512)(128)(4,1)S(1)} %get-tuple-element.43, pred[8]{0:T(512)(128)(4,1)S(1)} %get-tuple-element.40, pred[8]{0:T(512)(128)(4,1)S(1)} %get-tuple-element.37, ...), kind=kOutput, calls=%fused_computation.114 | convolution fusion | flops 8544256 | bytes 1081368 | tf_op jit(solution)/shard_map/nab,nbr->nar/dot_general | solution.py:75
  66.5 1.7 %fusion.92 = f32[4,32,512]{2,1,0:T(8,128)} fusion(bf16[3,32,512]{2,1,0:T(8,128)(2,1)S(1)} %collective-permute-done.5, bf16[4,32,512]{2,1,0:T(8,128)(2,1)S(1)} %bitcast_reduce_fusion.1, pred[4]{0:T(512)(128)(4,1)S(1)} %get-tuple-element.57, pred[4]{0:T(512)(128)(4,1)S(1)} %get-tuple-element.54, pred[4]{0:T(512)(128)(4,1)S(1)} %get-tuple-element.51, ...), kind=kOutput, calls=%fused_computation.129 | convolution fusion | flops 4272128 | bytes 589836 | tf_op jit(solution)/shard_map/nab,nbr->nar/dot_general | solution.py:75
  68.2 2.3 %fusion.63 = f32[16,32,512]{2,1,0:T(8,128)} fusion(bf16[16,32,512]{2,1,0:T(8,128)(2,1)S(1)} %convolution_convert_fusion, bf16[3,32,512]{2,1,0:T(8,128)(2,1)} %copy-done.15, pred[16]{0:T(512)(128)(4,1)S(1)} %get-tuple-element.32, pred[16]{0:T(512)(128)(4,1)S(1)} %get-tuple-element.29, pred[16]{0:T(512)(128)(4,1)S(1)} %get-tuple-element.26, ...), kind=kOutput, calls=%fused_computation.90 | convolution fusion | flops 17088512 | bytes 2064432 | tf_op jit(solution)/shard_map/nab,nbr->nar/dot_general | solution.py:75
  70.5 1.7 %fusion.88 = f32[4,32,512]{2,1,0:T(8,128)} fusion(bf16[4,32,512]{2,1,0:T(8,128)(2,1)S(1)} %bitcast_reduce_fusion.1, bf16[3,32,512]{2,1,0:T(8,128)(2,1)S(1)} %collective-permute-done.5, pred[4]{0:T(512)(128)(4,1)S(1)} %get-tuple-element.56, pred[4]{0:T(512)(128)(4,1)S(1)} %get-tuple-element.53, pred[4]{0:T(512)(128)(4,1)S(1)} %get-tuple-element.50, ...), kind=kOutput, calls=%fused_computation.126 | convolution fusion | flops 4272128 | bytes 589836 | tf_op jit(solution)/shard_map/nab,nbr->nar/dot_general | solution.py:75
  72.3 1.8 %fusion.94 = f32[4,32,512]{2,1,0:T(8,128)} fusion(bf16[4,32,512]{2,1,0:T(8,128)(2,1)S(1)} %bitcast_reduce_fusion.1, bf16[3,32,512]{2,1,0:T(8,128)(2,1)S(1)} %collective-permute-done.4, pred[4]{0:T(512)(128)(4,1)S(1)} %get-tuple-element.55, pred[4]{0:T(512)(128)(4,1)S(1)} %get-tuple-element.52, pred[4]{0:T(512)(128)(4,1)S(1)} %get-tuple-element.49, ...), kind=kOutput, calls=%fused_computation.132 | convolution fusion | flops 4272128 | bytes 589836 | tf_op jit(solution)/shard_map/nab,nbr->nar/dot_general | solution.py:75
  74.0 2.4 %fusion.70 = f32[16,32,512]{2,1,0:T(8,128)} fusion(bf16[16,32,512]{2,1,0:T(8,128)(2,1)S(1)} %convolution_convert_fusion, bf16[3,32,512]{2,1,0:T(8,128)(2,1)S(1)} %collective-permute-done, pred[16]{0:T(512)(128)(4,1)S(1)} %get-tuple-element.31, pred[16]{0:T(512)(128)(4,1)S(1)} %get-tuple-element.28, pred[16]{0:T(512)(128)(4,1)S(1)} %get-tuple-element.25, ...), kind=kOutput, calls=%fused_computation.96 | convolution fusion | flops 17088512 | bytes 2064432 | tf_op jit(solution)/shard_map/nab,nbr->nar/dot_general | solution.py:75
  76.4 3.6 %pad_maximum_fusion = (bf16[4096,512]{1,0:T(8,128)(2,1)}, bf16[4096,512]{1,0:T(8,128)(2,1)}) fusion(bf16[256,512]{1,0:T(8,128)(2,1)S(1)} %collective-permute-done.7, bf16[4096,512]{1,0:T(8,128)(2,1)S(1)} %copy-done.1, bf16[256,512]{1,0:T(8,128)(2,1)S(1)} %collective-permute-done.6), kind=kLoop, calls=%fused_computation.7 | loop fusion | flops 16777216 | bytes 13107200 | tf_op jit(solution)/shard_map/concatenate | solution.py:12
  80.1 2.8 %all-to-all-done = bf16[8,16,4096]{2,1,0:T(8,128)(2,1)} async-done(((bf16[8,16,4096]{2,1,0:T(8,128)(2,1)}), bf16[8,16,4096]{2,1,0:T(8,128)(2,1)}, u32[]{:S(2)}, u32[]{:S(2)}) %all-to-all-start) | async-done | bytes 1048608 | tf_op jit(solution)/shard_map/all_to_all | solution.py:25
  82.9 0.7 slice.455
  83.6 0.8 slice.456
  84.4 0.8 slice.453
  85.2 0.8 slice.454
  86.0 0.8 slice.451
  86.8 1.5 slice.452
  88.4 0.9 slice.449
  89.3 1.6 slice.450
  90.9 1.8 %slice.448 = bf16[64,3072]{1,0:T(8,128)(2,1)} slice(bf16[128,4096]{1,0:T(8,128)(2,1)} %bitcast.50), slice={[64:128], [1024:4096]} | slice | bytes 786432 | tf_op jit(solution)/shard_map/slice | solution.py:105
  92.7 0.7 slice.404
  93.4 0.8 slice.406
  94.3 0.9 copy.147
  95.2 0.9 slice.401
  96.2 1.7 %copy.157 = bf16[64,32,32]{2,1,0:T(8,128)(2,1)S(1)} copy(bf16[64,32,32]{0,2,1:T(8,128)(2,1)} %bitcast.567) | data formatting | bytes 262144 | tf_op jit(solution)/shard_map/slice | solution.py:111
  98.6 1.0 bitcast_reduce_fusion.6
  99.6 1.3 gather_fusion.3
  100.9 1.4 gather_fusion.2
  102.3 1.5 gather_fusion.1
  103.9 2.0 %slice.396 = bf16[16,3,32,32]{3,2,1,0:T(8,128)(2,1)} reshape(bf16[16,3072]{1,0:T(8,128)(2,1)} %slice.452) | data formatting | bytes 196608 | tf_op jit(solution)/shard_map/slice | solution.py:105
  105.9 2.2 %copy.141 = bf16[64,3072]{0,1:T(8,128)(2,1)} copy(bf16[64,3072]{1,0:T(8,128)(2,1)} %slice.448) | data formatting | bytes 786432 | tf_op jit(solution)/shard_map/slice | solution.py:105
  108.1 2.4 %slice.391 = bf16[32,3,32,32]{3,2,1,0:T(8,128)(2,1)} reshape(bf16[32,3072]{1,0:T(8,128)(2,1)} %slice.450) | data formatting | bytes 393216 | tf_op jit(solution)/shard_map/slice | solution.py:105
  110.5 3.1 %copy.146 = bf16[64,3,32,32]{3,2,1,0:T(8,128)(2,1)} copy(bf16[64,3,32,32]{0,3,2,1:T(8,128)(2,1)} %bitcast.563) | data formatting | bytes 786432 | tf_op jit(solution)/shard_map/slice | solution.py:105
  113.5 1.3 gather_fusion.4
  114.8 1.2 fusion.56
  116.1 1.2 convolution_bitcast_fusion.6
  117.3 1.0 fusion.55
  118.3 1.4 convolution_bitcast_fusion.5
  120.0 1.6 convolution_bitcast_fusion.4
  121.9 1.9 %convolution_bitcast_fusion.2 = f32[64,32,16]{1,2,0:T(8,128)S(1)} fusion(bf16[64,3,32,32]{3,2,1,0:T(8,128)(2,1)S(1)} %copy-done.3, bf16[64,3,32,16]{2,3,1,0:T(8,128)(2,1)} %bitcast.562, pred[64,3]{1,0:T(8,128)(4,1)S(1)} %copy-done.17), kind=kOutput, calls=%fused_computation.53 | convolution fusion | flops 6389760 | bytes 721088 | tf_op jit(solution)/shard_map/nsab,nsbr->nar/dot_general | solution.py:54
  124.2 0.9 reshape.484
  125.1 7.5 %all-to-all-start.2 = ((bf16[32,2,512]{2,1,0:T(2,128)(2,1)}), bf16[32,2,512]{2,1,0:T(2,128)(2,1)S(1)}, u32[]{:S(2)}, u32[]{:S(2)}) async-start(bf16[32,2,512]{2,1,0:T(2,128)(2,1)} %reshape.484), calls=%async_computation.2 | async-start | bytes 131072 | tf_op jit(solution)/shard_map/all_to_all | solution.py:167
  132.6 8.6 %fusion.3 = f32[16,256,512]{2,1,0:T(8,128)} fusion(bf16[16,256,512]{2,1,0:T(8,128)(2,1)} %bitcast.561, pred[16]{0:T(512)(128)(4,1)S(1)} %copy-done.31, pred[16]{0:T(512)(128)(4,1)S(1)} %copy-done.32, pred[16]{0:T(512)(128)(4,1)S(1)} %copy-done.33, bf16[16,3,256,256]{3,2,1,0:T(8,128)(2,1)} %param.12), kind=kOutput, calls=%fused_computation.14 | convolution fusion | flops 1076887552 | bytes 18874416 | tf_op jit(solution)/shard_map/npq,nqr->npr/dot_general | solution.py:143
  141.7 0.9 convolution_bitcast_fusion.3
  142.7 1.4 fusion.53
  144.1 1.0 convolution_bitcast_fusion.1
  145.2 1.6 fusion.48
  146.9 1.2 convolution_bitcast_fusion
  148.2 6.6 %fusion.46 = f32[16,512,256]{1,2,0:T(8,128)} fusion(bf16[16,256,32]{1,2,0:T(8,128)(2,1)S(1)} %copy-done, f32[16,32,512]{2,1,0:T(8,128)S(1)} %convolution_bitcast_fusion, f32[16,32,512]{2,1,0:T(8,128)S(1)} %fusion.68, f32[16,32,512]{2,1,0:T(8,128)} %fusion.63, f32[16,32,512]{2,1,0:T(8,128)} %fusion.70, bf16[3,32,512]{2,1,0:T(8,128)(2,1)S(1)} %copy-done.7, ...), kind=kOutput, calls=%fused_computation.58 | convolution fusion | flops 152616960 | bytes 13860912 | tf_op jit(solution)/shard_map/npk,nkr->npr/dot_general | solution.py:176
  154.8 15.3 %fusion = bf16[16,256,512]{2,1,0:T(8,128)(2,1)} fusion(f32[16,512,256]{1,2,0:T(8,128)} %fusion.46, f32[16,256,512]{2,1,0:T(8,128)} %fusion.3, f32[16,256,512]{2,1,0:T(8,128)} %fusion.7, bf16[16,256,512]{2,1,0:T(8,128)(2,1)} %bitcast.560, pred[16]{0:T(512)(128)(4,1)S(1)} %copy-done.30, pred[16]{0:T(512)(128)(4,1)S(1)} %copy-done.29, ...), kind=kOutput, calls=%fused_computation.6 | convolution fusion | flops 1085276160 | bytes 39845936 | tf_op jit(solution)/shard_map/npq,nqr->npr/dot_general | solution.py:143
  (179 shorter events, 18.2 us)
Async XLA Ops:
  0.0 148.1 %copy-start = (bf16[16,256,32]{1,2,0:T(8,128)(2,1)S(1)}, bf16[16,256,32]{1,2,0:T(8,128)(2,1)}, u32[]{:S(2)}) copy-start(bf16[16,256,32]{1,2,0:T(8,128)(2,1)} %param.15) | copy-start | bytes 786436
  0.0 6.6 %copy-start.5 = (bf16[28,32,32]{2,1,0:T(8,128)(2,1)S(1)}, bf16[28,32,32]{2,1,0:T(8,128)(2,1)}, u32[]{:S(2)}) copy-start(bf16[28,32,32]{2,1,0:T(8,128)(2,1)} %param.16) | copy-start | bytes 172036
  0.0 26.0 %copy-start.13 = (s32[128,3]{0,1:T(4,128)S(1)}, s32[128,3]{0,1:T(4,128)}, u32[]{:S(2)}) copy-start(s32[128,3]{0,1:T(4,128)} %param.21) | copy-start | bytes 4612
  3.1 27.4 %copy-start.16 = (s32[28,3]{0,1:T(4,128)S(1)}, s32[28,3]{0,1:T(4,128)}, u32[]{:S(2)}) copy-start(s32[28,3]{0,1:T(4,128)} %param.20) | copy-start | bytes 1012
  3.2 28.6 %copy-start.24 = (s32[16,3]{0,1:T(4,128)S(1)}, s32[16,3]{0,1:T(4,128)}, u32[]{:S(2)}) copy-start(s32[16,3]{0,1:T(4,128)} %param.13) | copy-start | bytes 580
  3.2 32.3 %copy-start.14 = (bf16[16,32,32]{2,1,0:T(8,128)(2,1)S(1)}, bf16[16,32,32]{2,1,0:T(8,128)(2,1)}, u32[]{:S(2)}) copy-start(bf16[16,32,32]{2,1,0:T(8,128)(2,1)} %param.17) | copy-start | bytes 98308
  3.2 32.5 %copy-start.12 = (bf16[16,3,32,32]{3,2,1,0:T(8,128)(2,1)S(1)}, bf16[16,3,32,32]{3,2,1,0:T(8,128)(2,1)}, u32[]{:S(2)}) copy-start(bf16[16,3,32,32]{3,2,1,0:T(8,128)(2,1)} %param.19) | copy-start | bytes 294916
  3.2 70.8 %collective-permute-start = (bf16[3,32,512]{2,1,0:T(8,128)(2,1)S(1)}, bf16[3,32,512]{2,1,0:T(8,128)(2,1)S(1)}, u32[]{:S(2)}, u32[]{:S(2)}) collective-permute-start(bf16[3,32,512]{2,1,0:T(8,128)(2,1)S(1)} %get-tuple-element.9), channel_id=1, source_target_pairs={{0,8},{8,16},{16,24},{24,32},{32,40},{40,48},{48,56},{56,64},{64,7... | collective-permute-start | bytes 294920 | tf_op jit(solution)/shard_map/ppermute | solution.py:14
  5.9 53.3 %collective-permute-start.1 = (bf16[3,32,512]{2,1,0:T(8,128)(2,1)S(1)}, bf16[3,32,512]{2,1,0:T(8,128)(2,1)S(1)}, u32[]{:S(2)}, u32[]{:S(2)}) collective-permute-start(bf16[3,32,512]{2,1,0:T(8,128)(2,1)S(1)} %get-tuple-element.10), channel_id=1, source_target_pairs={{8,0},{16,8},{24,16},{32,24},{40,32},{48,40},{56,48},{64,56},{72,6... | collective-permute-start | bytes 294920 | tf_op jit(solution)/shard_map/ppermute | solution.py:16
  7.9 64.3 %collective-permute-start.4 = (bf16[3,32,512]{2,1,0:T(8,128)(2,1)}, bf16[3,32,512]{2,1,0:T(8,128)(2,1)S(1)}, u32[]{:S(2)}, u32[]{:S(2)}) collective-permute-start(bf16[3,32,512]{2,1,0:T(8,128)(2,1)} %get-tuple-element.13), channel_id=1, source_target_pairs={{0,8},{8,16},{16,24},{24,32},{32,40},{40,48},{48,56},{56,64},{64,7... | collective-permute-start | bytes 294920 | tf_op jit(solution)/shard_map/ppermute | solution.py:14
  9.0 57.5 %collective-permute-start.5 = (bf16[3,32,512]{2,1,0:T(8,128)(2,1)}, bf16[3,32,512]{2,1,0:T(8,128)(2,1)S(1)}, u32[]{:S(2)}, u32[]{:S(2)}) collective-permute-start(bf16[3,32,512]{2,1,0:T(8,128)(2,1)} %get-tuple-element.14), channel_id=1, source_target_pairs={{8,0},{16,8},{24,16},{32,24},{40,32},{48,40},{56,48},{64,56},{72,6... | collective-permute-start | bytes 294920 | tf_op jit(solution)/shard_map/ppermute | solution.py:16
  13.5 41.8 %collective-permute-start.3 = (bf16[3,32,512]{2,1,0:T(8,128)(2,1)S(1)}, bf16[3,32,512]{2,1,0:T(8,128)(2,1)S(1)}, u32[]{:S(2)}, u32[]{:S(2)}) collective-permute-start(bf16[3,32,512]{2,1,0:T(8,128)(2,1)S(1)} %get-tuple-element.12), channel_id=1, source_target_pairs={{8,0},{16,8},{24,16},{32,24},{40,32},{48,40},{56,48},{64,56},{72,6... | collective-permute-start | bytes 294920 | tf_op jit(solution)/shard_map/ppermute | solution.py:16
  22.4 23.6 %all-to-all-start.1 = ((bf16[32,2,512]{2,1,0:T(2,128)(2,1)}), bf16[32,2,512]{2,1,0:T(2,128)(2,1)S(1)}, u32[]{:S(2)}, u32[]{:S(2)}) async-start(bf16[32,2,512]{2,1,0:T(2,128)(2,1)} %reshape.482), calls=%async_computation.1 | async-start | bytes 131072 | tf_op jit(solution)/shard_map/all_to_all | solution.py:158
  47.1 35.8 %all-to-all-start = ((bf16[8,16,4096]{2,1,0:T(8,128)(2,1)}), bf16[8,16,4096]{2,1,0:T(8,128)(2,1)}, u32[]{:S(2)}, u32[]{:S(2)}) async-start(bf16[8,16,4096]{2,1,0:T(8,128)(2,1)} %broadcast_in_dim.421), calls=%async_computation | async-start | bytes 2097152 | tf_op jit(solution)/shard_map/all_to_all | solution.py:25
  55.4 8.0 %collective-permute-start.2 = (bf16[3,32,512]{2,1,0:T(8,128)(2,1)}, bf16[3,32,512]{2,1,0:T(8,128)(2,1)S(1)}, u32[]{:S(2)}, u32[]{:S(2)}) collective-permute-start(bf16[3,32,512]{2,1,0:T(8,128)(2,1)} %get-tuple-element.11), channel_id=1, source_target_pairs={{0,8},{8,16},{16,24},{24,32},{32,40},{40,48},{48,56},{56,64},{64,7... | collective-permute-start | bytes 294920 | tf_op jit(solution)/shard_map/ppermute | solution.py:14
  59.2 0.6 copy-start.15
  59.2 17.3 %collective-permute-start.7 = (bf16[256,512]{1,0:T(8,128)(2,1)}, bf16[256,512]{1,0:T(8,128)(2,1)S(1)}, u32[]{:S(2)}, u32[]{:S(2)}) collective-permute-start(bf16[256,512]{1,0:T(8,128)(2,1)} %get-tuple-element.7), channel_id=1, source_target_pairs={{8,0},{16,8},{24,16},{32,24},{40,32},{48,40},{56,48},{64,56},{72,6... | collective-permute-start | bytes 786440 | tf_op jit(solution)/shard_map/ppermute | solution.py:16
  59.8 16.7 %copy-start.1 = (bf16[4096,512]{1,0:T(8,128)(2,1)S(1)}, bf16[4096,512]{1,0:T(8,128)(2,1)}, u32[]{:S(2)}) copy-start(bf16[4096,512]{1,0:T(8,128)(2,1)} %param.11) | copy-start | bytes 12582916
  63.4 16.7 %copy-start.8 = (bf16[3,32,512]{2,1,0:T(8,128)(2,1)}, bf16[3,32,512]{2,1,0:T(8,128)(2,1)S(1)}, u32[]{:S(2)}) copy-start(bf16[3,32,512]{2,1,0:T(8,128)(2,1)S(1)} %collective-permute-done.2) | copy-start | bytes 294916
  63.4 13.1 %collective-permute-start.6 = (bf16[256,512]{1,0:T(8,128)(2,1)}, bf16[256,512]{1,0:T(8,128)(2,1)S(1)}, u32[]{:S(2)}, u32[]{:S(2)}) collective-permute-start(bf16[256,512]{1,0:T(8,128)(2,1)} %get-tuple-element.8), channel_id=1, source_target_pairs={{0,8},{8,16},{16,24},{24,32},{32,40},{40,48},{48,56},{56,64},{64,7... | collective-permute-start | bytes 786440 | tf_op jit(solution)/shard_map/ppermute | solution.py:14
  72.3 7.8 %copy-start.10 = (bf16[3,32,512]{2,1,0:T(8,128)(2,1)}, bf16[3,32,512]{2,1,0:T(8,128)(2,1)S(1)}, u32[]{:S(2)}) copy-start(bf16[3,32,512]{2,1,0:T(8,128)(2,1)S(1)} %collective-permute-done.4) | copy-start | bytes 294916
  74.0 6.1 %copy-start.6 = (bf16[3,32,512]{2,1,0:T(8,128)(2,1)}, bf16[3,32,512]{2,1,0:T(8,128)(2,1)S(1)}, u32[]{:S(2)}) copy-start(bf16[3,32,512]{2,1,0:T(8,128)(2,1)S(1)} %collective-permute-done) | copy-start | bytes 294916
  103.9 16.1 %copy-start.4 = (bf16[96,32,16]{1,2,0:T(8,128)(2,1)S(1)}, bf16[96,32,16]{1,2,0:T(8,128)(2,1)}, u32[]{:S(2)}) copy-start(bf16[96,32,16]{1,2,0:T(8,128)(2,1)} %gather_fusion.1) | copy-start | bytes 294916
  114.8 7.0 %copy-start.3 = (bf16[64,3,32,32]{3,2,1,0:T(8,128)(2,1)S(1)}, bf16[64,3,32,32]{3,2,1,0:T(8,128)(2,1)}, u32[]{:S(2)}) copy-start(bf16[64,3,32,32]{3,2,1,0:T(8,128)(2,1)} %copy.146) | copy-start | bytes 1179652
  114.8 7.0 %copy-start.17 = (pred[64,3]{1,0:T(8,128)(4,1)S(1)}, pred[64,3]{1,0:T(8,128)(4,1)}, u32[]{:S(2)}) copy-start(pred[64,3]{1,0:T(8,128)(4,1)} %copy.142) | copy-start | bytes 580
  119.8 12.8 %copy-start.31 = (pred[16]{0:T(512)(128)(4,1)S(1)}, pred[16]{0:T(512)(128)(4,1)}, u32[]{:S(2)}) copy-start(pred[16]{0:T(512)(128)(4,1)} %get-tuple-element.21) | copy-start | bytes 52
  119.8 12.8 %copy-start.32 = (pred[16]{0:T(512)(128)(4,1)S(1)}, pred[16]{0:T(512)(128)(4,1)}, u32[]{:S(2)}) copy-start(pred[16]{0:T(512)(128)(4,1)} %get-tuple-element.22) | copy-start | bytes 52
  119.8 12.8 %copy-start.33 = (pred[16]{0:T(512)(128)(4,1)S(1)}, pred[16]{0:T(512)(128)(4,1)}, u32[]{:S(2)}) copy-start(pred[16]{0:T(512)(128)(4,1)} %get-tuple-element.23) | copy-start | bytes 52
  125.1 16.2 %all-to-all-start.2 = ((bf16[32,2,512]{2,1,0:T(2,128)(2,1)}), bf16[32,2,512]{2,1,0:T(2,128)(2,1)S(1)}, u32[]{:S(2)}, u32[]{:S(2)}) async-start(bf16[32,2,512]{2,1,0:T(2,128)(2,1)} %reshape.484), calls=%async_computation.2 | async-start | bytes 131072 | tf_op jit(solution)/shard_map/all_to_all | solution.py:167
  132.6 10.1 %copy-start.11 = (bf16[3,32,512]{2,1,0:T(8,128)(2,1)S(1)}, bf16[3,32,512]{2,1,0:T(8,128)(2,1)}, u32[]{:S(2)}) copy-start(bf16[3,32,512]{2,1,0:T(8,128)(2,1)} %copy-done.10) | copy-start | bytes 294916
  132.6 10.1 %copy-start.21 = (pred[4]{0:T(512)(128)(4,1)S(1)}, pred[4]{0:T(512)(128)(4,1)}, u32[]{:S(2)}) copy-start(pred[4]{0:T(512)(128)(4,1)} %get-tuple-element.48) | copy-start | bytes 16
  132.6 10.1 %copy-start.22 = (pred[4]{0:T(512)(128)(4,1)S(1)}, pred[4]{0:T(512)(128)(4,1)}, u32[]{:S(2)}) copy-start(pred[4]{0:T(512)(128)(4,1)} %get-tuple-element.58) | copy-start | bytes 16
  132.6 10.1 %copy-start.23 = (pred[4]{0:T(512)(128)(4,1)S(1)}, pred[4]{0:T(512)(128)(4,1)}, u32[]{:S(2)}) copy-start(pred[4]{0:T(512)(128)(4,1)} %get-tuple-element.59) | copy-start | bytes 16
  141.3 3.9 %copy-start.2 = (f32[8,32,512]{2,1,0:T(8,128)S(1)}, f32[8,32,512]{2,1,0:T(8,128)}, u32[]{:S(2)}) copy-start(f32[8,32,512]{2,1,0:T(8,128)} %fusion.80) | copy-start | bytes 1572868
  141.3 3.9 %copy-start.9 = (bf16[3,32,512]{2,1,0:T(8,128)(2,1)S(1)}, bf16[3,32,512]{2,1,0:T(8,128)(2,1)}, u32[]{:S(2)}) copy-start(bf16[3,32,512]{2,1,0:T(8,128)(2,1)} %copy-done.8) | copy-start | bytes 294916
  141.3 3.9 %copy-start.25 = (pred[8]{0:T(512)(128)(4,1)S(1)}, pred[8]{0:T(512)(128)(4,1)}, u32[]{:S(2)}) copy-start(pred[8]{0:T(512)(128)(4,1)} %get-tuple-element.36) | copy-start | bytes 28
  141.3 4.0 %copy-start.26 = (pred[8]{0:T(512)(128)(4,1)S(1)}, pred[8]{0:T(512)(128)(4,1)}, u32[]{:S(2)}) copy-start(pred[8]{0:T(512)(128)(4,1)} %get-tuple-element.46) | copy-start | bytes 28
  141.3 4.0 %copy-start.27 = (pred[8]{0:T(512)(128)(4,1)S(1)}, pred[8]{0:T(512)(128)(4,1)}, u32[]{:S(2)}) copy-start(pred[8]{0:T(512)(128)(4,1)} %get-tuple-element.47) | copy-start | bytes 28
  141.6 6.5 %copy-start.7 = (bf16[3,32,512]{2,1,0:T(8,128)(2,1)S(1)}, bf16[3,32,512]{2,1,0:T(8,128)(2,1)}, u32[]{:S(2)}) copy-start(bf16[3,32,512]{2,1,0:T(8,128)(2,1)} %copy-done.6) | copy-start | bytes 294916
  141.6 6.5 %copy-start.18 = (pred[16]{0:T(512)(128)(4,1)S(1)}, pred[16]{0:T(512)(128)(4,1)}, u32[]{:S(2)}) copy-start(pred[16]{0:T(512)(128)(4,1)} %get-tuple-element.24) | copy-start | bytes 52
  141.7 6.5 %copy-start.19 = (pred[16]{0:T(512)(128)(4,1)S(1)}, pred[16]{0:T(512)(128)(4,1)}, u32[]{:S(2)}) copy-start(pred[16]{0:T(512)(128)(4,1)} %get-tuple-element.34) | copy-start | bytes 52
  141.7 6.5 %copy-start.20 = (pred[16]{0:T(512)(128)(4,1)S(1)}, pred[16]{0:T(512)(128)(4,1)}, u32[]{:S(2)}) copy-start(pred[16]{0:T(512)(128)(4,1)} %get-tuple-element.35) | copy-start | bytes 52
  148.1 6.6 %copy-start.28 = (pred[16]{0:T(512)(128)(4,1)S(1)}, pred[16]{0:T(512)(128)(4,1)}, u32[]{:S(2)}) copy-start(pred[16]{0:T(512)(128)(4,1)} %get-tuple-element.15) | copy-start | bytes 52
  148.1 6.6 %copy-start.29 = (pred[16]{0:T(512)(128)(4,1)S(1)}, pred[16]{0:T(512)(128)(4,1)}, u32[]{:S(2)}) copy-start(pred[16]{0:T(512)(128)(4,1)} %get-tuple-element.18) | copy-start | bytes 52
  148.2 6.6 %copy-start.30 = (pred[16]{0:T(512)(128)(4,1)S(1)}, pred[16]{0:T(512)(128)(4,1)}, u32[]{:S(2)}) copy-start(pred[16]{0:T(512)(128)(4,1)} %get-tuple-element.20) | copy-start | bytes 52
